TPU v7x, 32 devices: a whole 2x2x4 slice. The times are simulated.
32 devices in a mesh: replica: 16 (over z, x, core), group: 2 (over y).
Axes of the slice: x: 2, y: 2, z: 4, core: 2. Of those that a mesh axis runs over, the one named last changes fastest.
Arguments:
- inputs: bfloat16 [640, 197, 384], P(('replica', 'group')), may hold values from -6 to 6
- cotangent: bfloat16 [640, 197, 384], P(('replica', 'group')), may hold values from -6 to 6
- gain_one: bfloat16 [384], P('group'), may hold values from 0.5 to 1.5
- shift_one: bfloat16 [384], P('group'), may hold values from -3 to 3
- w_qkv: bfloat16 [384, 1152], P('group'), may hold values from -2 to 2
- b_query: bfloat16 [384], P('group'), may hold values from -3 to 3
- b_value: bfloat16 [384], P('group'), may hold values from -3 to 3
- w_proj: bfloat16 [384, 384], P('group'), may hold values from -0.875 to 0.875
- b_proj: bfloat16 [384], P('group'), may hold values from -3 to 3
- gain_two: bfloat16 [384], P('group'), may hold values from 0.5 to 1.5
- shift_two: bfloat16 [384], P('group'), may hold values from -3 to 3
- w_fc1: bfloat16 [384, 1536], P('group'), may hold values from -0.3125 to 0.3125
- b_fc1: bfloat16 [1536], P('group'), may hold values from -3 to 3
- w_fc2: bfloat16 [1536, 384], P('group'), may hold values from -0.15625 to 0.15625
- b_fc2: bfloat16 [384], P('group'), may hold values from -3 to 3
Outputs:
- outputs: bfloat16 [640, 197, 384], P(('replica', 'group'))
- grad_inputs: float32 [640, 197, 384], P(('replica', 'group'))
- grad_gain_one: float32 [384], P('group')
- grad_shift_one: float32 [384], P('group')
- grad_w_qkv: float32 [384, 1152], P('group')
- grad_b_query: float32 [384], P('group')
- grad_b_value: float32 [384], P('group')
- grad_w_proj: float32 [384, 384], P('group')
- grad_b_proj: float32 [384], P('group')
- grad_gain_two: float32 [384], P('group')
- grad_shift_two: float32 [384], P('group')
- grad_w_fc1: float32 [384, 1536], P('group')
- grad_b_fc1: float32 [1536], P('group')
- grad_w_fc2: float32 [1536, 384], P('group')
- grad_b_fc2: float32 [384], P('group')
All inputs are finite; a program needn't handle non-finite values.
Results may differ from a plain program's by a relative error of at most 0.012.
Values may be sent and summed in bfloat16 or wider, within the bound.
A program may use at most 256 MiB of HBM per device.

v0:
```python
import jax
import jax.numpy as jnp
from jax import lax
from jax.sharding import PartitionSpec as P

HEADS = 6
epsilon = 1e-06


def product(left, right):
    return jnp.dot(left, right, preferred_element_type=jnp.float32)


def product_left_t(left, right):
    return lax.dot_general(
        left, right, (((0,), (0,)), ((), ())), preferred_element_type=jnp.float32
    )


def product_right_t(left, right):
    return lax.dot_general(
        left, right, (((1,), (1,)), ((), ())), preferred_element_type=jnp.float32
    )


def layer_norm(token_rows, gain_row, shift_row):
    centre = jnp.mean(token_rows, axis=-1, keepdims=True)
    centered = token_rows - centre
    inverse = lax.rsqrt(jnp.mean(centered * centered, axis=-1, keepdims=True) + epsilon)
    normed = centered * inverse
    hidden = (normed * gain_row.astype(jnp.float32) + shift_row.astype(jnp.float32)).astype(
        jnp.bfloat16
    )
    return (normed, inverse, hidden)


def norm_backward(grad_hidden, normed, inverse, gain_row):
    grad_normed = grad_hidden * gain_row.astype(jnp.float32)
    average_one = jnp.mean(grad_normed, axis=-1, keepdims=True)
    average_two = jnp.mean(grad_normed * normed, axis=-1, keepdims=True)
    grad_rows = inverse * (grad_normed - average_one - normed * average_two)
    return (grad_rows, jnp.sum(grad_hidden * normed, axis=0), jnp.sum(grad_hidden, axis=0))


def gelu_slope(values):
    return (
        0.5 * (1.0 + lax.erf(values * 0.7071067811865476))
        + values * jnp.exp(-0.5 * values * values) * 0.3989422804014327
    )


def attention_scores(query, keys, scaling):
    return jnp.einsum("bshe,bthe->bhst", query, keys, preferred_element_type=jnp.float32) * scaling


def forward_pass(inputs, params):
    (
        gain_one,
        shift_one,
        w_qkv,
        b_query,
        b_value,
        w_proj,
        b_proj,
        gain_two,
        shift_two,
        w_fc1,
        b_fc1,
        w_fc2,
        b_fc2,
    ) = params
    images, length, width = inputs.shape
    head_dim = width // HEADS
    scaling = head_dim ** (-0.5)
    row_count = images * length
    token_rows = inputs.reshape(row_count, width).astype(jnp.float32)
    normed_one, inverse_one, hidden_one = layer_norm(token_rows, gain_one, shift_one)
    bias_full = jnp.concatenate([b_query, jnp.zeros_like(b_query), b_value]).astype(jnp.float32)
    packed = (product(hidden_one, w_qkv) + bias_full).astype(jnp.bfloat16)
    packed = packed.reshape(images, length, 3, HEADS, head_dim)
    query = packed[:, :, 0]
    keys = packed[:, :, 1]
    values = packed[:, :, 2]
    scores = attention_scores(query, keys, scaling)
    log_total = jax.nn.logsumexp(scores, axis=-1, keepdims=True)
    probs_b = jnp.exp(scores - log_total).astype(jnp.bfloat16)
    attended = jnp.einsum("bhst,bthe->bshe", probs_b, values, preferred_element_type=jnp.float32)
    attended = attended.astype(jnp.bfloat16).reshape(row_count, width)
    resid = token_rows + product(attended, w_proj) + b_proj.astype(jnp.float32)
    normed_two, inverse_two, hidden_two = layer_norm(resid, gain_two, shift_two)
    pre_act = product(hidden_two, w_fc1) + b_fc1.astype(jnp.float32)
    act_b = jax.nn.gelu(pre_act, approximate=False).astype(jnp.bfloat16)
    outputs = (resid + product(act_b, w_fc2) + b_fc2.astype(jnp.float32)).astype(jnp.bfloat16)
    saved = (
        normed_one,
        inverse_one,
        hidden_one,
        query,
        keys,
        values,
        log_total,
        attended,
        normed_two,
        inverse_two,
        hidden_two,
        pre_act,
        act_b,
    )
    return (outputs.reshape(images, length, width), saved)


def backward_pass(cotangent, saved, params):
    (
        gain_one,
        shift_one,
        w_qkv,
        b_query,
        b_value,
        w_proj,
        b_proj,
        gain_two,
        shift_two,
        w_fc1,
        b_fc1,
        w_fc2,
        b_fc2,
    ) = params
    (
        normed_one,
        inverse_one,
        hidden_one,
        query,
        keys,
        values,
        log_total,
        attended,
        normed_two,
        inverse_two,
        hidden_two,
        pre_act,
        act_b,
    ) = saved
    images, length, width = cotangent.shape
    head_dim = width // HEADS
    scaling = head_dim ** (-0.5)
    row_count = images * length
    grad_out = cotangent.reshape(row_count, width)
    grad_top = grad_out.astype(jnp.float32)
    grad_b_fc2 = jnp.sum(grad_top, axis=0)
    grad_w_fc2 = product_left_t(act_b, grad_out)
    grad_pre = product_right_t(grad_out, w_fc2) * gelu_slope(pre_act)
    grad_b_fc1 = jnp.sum(grad_pre, axis=0)
    grad_pre_b = grad_pre.astype(jnp.bfloat16)
    grad_w_fc1 = product_left_t(hidden_two, grad_pre_b)
    grad_hidden_two = product_right_t(grad_pre_b, w_fc1)
    grad_part, grad_gain_two, grad_shift_two = norm_backward(
        grad_hidden_two, normed_two, inverse_two, gain_two
    )
    grad_resid = grad_top + grad_part
    grad_b_proj = jnp.sum(grad_resid, axis=0)
    grad_resid_b = grad_resid.astype(jnp.bfloat16)
    grad_w_proj = product_left_t(attended, grad_resid_b)
    grad_attended = product_right_t(grad_resid_b, w_proj).astype(jnp.bfloat16)
    grad_attended = grad_attended.reshape(images, length, HEADS, head_dim)
    probs = jnp.exp(attention_scores(query, keys, scaling) - log_total)
    probs_b = probs.astype(jnp.bfloat16)
    grad_values = jnp.einsum(
        "bhst,bshe->bthe", probs_b, grad_attended, preferred_element_type=jnp.float32
    )
    grad_probs = jnp.einsum(
        "bshe,bthe->bhst", grad_attended, values, preferred_element_type=jnp.float32
    )
    delta_rows = jnp.sum(probs * grad_probs, axis=-1, keepdims=True)
    grad_scores = (probs * (grad_probs - delta_rows) * scaling).astype(jnp.bfloat16)
    grad_query = jnp.einsum(
        "bhst,bthe->bshe", grad_scores, keys, preferred_element_type=jnp.float32
    )
    grad_keys = jnp.einsum(
        "bhst,bshe->bthe", grad_scores, query, preferred_element_type=jnp.float32
    )
    grad_b_query = jnp.sum(grad_query.reshape(row_count, width), axis=0)
    grad_b_value = jnp.sum(grad_values.reshape(row_count, width), axis=0)
    grad_packed_b = (
        jnp.stack([grad_query, grad_keys, grad_values], axis=2)
        .reshape(row_count, 3 * width)
        .astype(jnp.bfloat16)
    )
    grad_w_qkv = product_left_t(hidden_one, grad_packed_b)
    grad_hidden_one = product_right_t(grad_packed_b, w_qkv)
    grad_first, grad_gain_one, grad_shift_one = norm_backward(
        grad_hidden_one, normed_one, inverse_one, gain_one
    )
    grad_inputs = (grad_resid + grad_first).reshape(images, length, width)
    grads = (
        grad_gain_one,
        grad_shift_one,
        grad_w_qkv,
        grad_b_query,
        grad_b_value,
        grad_w_proj,
        grad_b_proj,
        grad_gain_two,
        grad_shift_two,
        grad_w_fc1,
        grad_b_fc1,
        grad_w_fc2,
        grad_b_fc2,
    )
    return (grad_inputs, grads)


def owned_rows(whole, position, members):
    share = whole.shape[0] // members
    return lax.dynamic_slice_in_dim(whole, position * share, share, 0)


def local(
    inputs,
    cotangent,
    gain_one,
    shift_one,
    w_qkv,
    b_query,
    b_value,
    w_proj,
    b_proj,
    gain_two,
    shift_two,
    w_fc1,
    b_fc1,
    w_fc2,
    b_fc2,
):
    gathered = (
        lax.all_gather(gain_one, "group", axis=0, tiled=True),
        lax.all_gather(shift_one, "group", axis=0, tiled=True),
        lax.all_gather(w_qkv, "group", axis=0, tiled=True),
        lax.all_gather(b_query, "group", axis=0, tiled=True),
        lax.all_gather(b_value, "group", axis=0, tiled=True),
        lax.all_gather(w_proj, "group", axis=0, tiled=True),
        lax.all_gather(b_proj, "group", axis=0, tiled=True),
        lax.all_gather(gain_two, "group", axis=0, tiled=True),
        lax.all_gather(shift_two, "group", axis=0, tiled=True),
        lax.all_gather(w_fc1, "group", axis=0, tiled=True),
        lax.all_gather(b_fc1, "group", axis=0, tiled=True),
        lax.all_gather(w_fc2, "group", axis=0, tiled=True),
        lax.all_gather(b_fc2, "group", axis=0, tiled=True),
    )
    outputs, saved = forward_pass(inputs, gathered)
    params_back = (
        lax.all_gather(gain_one, "group", axis=0, tiled=True),
        lax.all_gather(shift_one, "group", axis=0, tiled=True),
        lax.all_gather(w_qkv, "group", axis=0, tiled=True),
        lax.all_gather(b_query, "group", axis=0, tiled=True),
        lax.all_gather(b_value, "group", axis=0, tiled=True),
        lax.all_gather(w_proj, "group", axis=0, tiled=True),
        lax.all_gather(b_proj, "group", axis=0, tiled=True),
        lax.all_gather(gain_two, "group", axis=0, tiled=True),
        lax.all_gather(shift_two, "group", axis=0, tiled=True),
        lax.all_gather(w_fc1, "group", axis=0, tiled=True),
        lax.all_gather(b_fc1, "group", axis=0, tiled=True),
        lax.all_gather(w_fc2, "group", axis=0, tiled=True),
        lax.all_gather(b_fc2, "group", axis=0, tiled=True),
    )
    grad_inputs, grads = backward_pass(cotangent, saved, params_back)
    (
        term_gain_one,
        term_shift_one,
        term_w_qkv,
        term_b_query,
        term_b_value,
        term_w_proj,
        term_b_proj,
        term_gain_two,
        term_shift_two,
        term_w_fc1,
        term_b_fc1,
        term_w_fc2,
        term_b_fc2,
    ) = grads
    wholes = lax.psum(
        (
            term_gain_one,
            term_shift_one,
            term_w_qkv,
            term_b_query,
            term_b_value,
            term_w_proj,
            term_b_proj,
            term_gain_two,
            term_shift_two,
            term_w_fc1,
            term_b_fc1,
            term_w_fc2,
            term_b_fc2,
        ),
        ("replica", "group"),
    )
    position = lax.axis_index("group")
    members = lax.axis_size("group")
    totals = tuple((owned_rows(whole, position, members) for whole in wholes))
    token_total = (
        inputs.shape[0] * inputs.shape[1] * lax.axis_size("replica") * lax.axis_size("group")
    )
    factor = float(token_total) ** (-0.5)
    return (outputs, grad_inputs) + tuple((total * factor for total in totals))


def solution(mesh):
    return jax.shard_map(
        local,
        mesh=mesh,
        in_specs=(
            P(("replica", "group"), None, None),
            P(("replica", "group"), None, None),
            P("group"),
            P("group"),
            P("group", None),
            P("group"),
            P("group"),
            P("group", None),
            P("group"),
            P("group"),
            P("group"),
            P("group", None),
            P("group"),
            P("group", None),
            P("group"),
        ),
        out_specs=(
            P(("replica", "group"), None, None),
            P(("replica", "group"), None, None),
            P("group"),
            P("group"),
            P("group", None),
            P("group"),
            P("group"),
            P("group", None),
            P("group"),
            P("group"),
            P("group"),
            P("group", None),
            P("group"),
            P("group", None),
            P("group"),
        ),
        check_vma=False,
    )
```

profile of v0, /device:TPU:0, one launch (start us, length us, event | category | flops | bytes accessed | tf_op | source)
XLA Modules:
  0.0 717.0 jit_solution(14712015260770157017)
XLA Ops:
  8.7 2.6 convert_reduce_fusion.1
  13.7 3.3 reshape.192
  17.1 4.4 reshape.189
  21.5 3.0 convert_reduce_fusion
  41.6 6.7 all-reduce.10
  53.7 15.1 %all_gather.47 = bf16[384,1152]{1,0:T(8,128)(2,1)S(1)} all-gather(bf16[192,1152]{1,0:T(8,128)(2,1)S(1)} %copy-done.18), channel_id=1, replica_groups=mesh['replica'=16,'group'=2] {'group'}, dimensions={0}, use_global_device_ids=true | all-gather | bytes 1327104 | tf_op jit(solution)/shard_map/all_gather | solution.py:237
  68.8 3.3 add_convert_fusion
  72.2 8.7 %fusion.17 = bf16[3940,1152]{1,0:T(8,128)(2,1)} fusion(bf16[384,1152]{1,0:T(8,128)(2,1)S(1)} %all_gather.47, f32[1152]{0:T(1024)S(1)} %maximum_convert_fusion.1, f32[3940,384]{1,0:T(8,128)S(1)} %copy-done.1, f32[384]{0:T(512)S(1)} %copy-done.27, f32[384]{0:T(512)S(1)} %copy-done.25, f32[3940]{0:T(1024)S(1)} %copy-done.23, f32[3940]{0:T(1024)S(1)} %div.27), kind=kOutput, calls=%fused_computation.34 | convolution fusion | flops 3502502400 | bytes 16053536 | tf_op jit(solution)/shard_map/dot_general | solution.py:11
  80.9 27.6 %reshape.236 = bf16[20,197,3,6,64]{4,3,2,1,0:T(8,128)(2,1)} reshape(bf16[3940,1152]{1,0:T(8,128)(2,1)} %fusion.17) | data formatting | bytes 18155520 | tf_op jit(solution)/shard_map/reshape | solution.py:80
  108.5 16.3 %fusion.67 = (bf16[20,197,1,6,64]{4,3,2,1,0:T(8,128)(2,1)}, bf16[20,197,1,6,64]{4,3,2,1,0:T(8,128)(2,1)}, bf16[20,197,1,6,64]{4,3,2,1,0:T(8,128)(2,1)}) fusion(bf16[20,197,3,6,64]{4,3,2,1,0:T(8,128)(2,1)} %reshape.236), kind=kLoop, calls=%fused_computation.116 | loop fusion | bytes 18155520 | tf_op jit(solution)/shard_map/slice | solution.py:81
  124.8 9.7 %copy.74 = bf16[20,197,1,6,64]{1,4,3,0,2:T(8,128)(2,1)} copy(bf16[20,197,1,6,64]{4,3,2,1,0:T(8,128)(2,1)} %get-tuple-element.46) | data formatting | bytes 6051840
  134.5 9.7 %copy.75 = bf16[20,197,1,6,64]{1,4,3,0,2:T(8,128)(2,1)} copy(bf16[20,197,1,6,64]{4,3,2,1,0:T(8,128)(2,1)} %get-tuple-element.48) | data formatting | bytes 6051840
  144.2 14.9 %multiply_reduce_fusion.1 = (f32[20,6,197]{2,1,0:T(8,128)S(1)}, f32[20,6,197,197]{2,3,1,0:T(8,128)}) fusion(bf16[20,197,1,6,64]{1,4,3,0,2:T(8,128)(2,1)} %copy.75, bf16[20,197,1,6,64]{1,4,3,0,2:T(8,128)(2,1)} %copy.74), kind=kOutput, calls=%fused_computation.32 | convolution fusion | flops 605396736 | bytes 24774720 | tf_op jit(solution)/shard_map/bshe,bthe->bhst/dot_general | solution.py:53
  159.2 10.6 %exponential_reduce_fusion = f32[20,6,197]{2,1,0:T(8,128)S(1)} fusion(f32[20,6,197,197]{2,3,1,0:T(8,128)} %get-tuple-element.50, f32[20,6,197]{2,1,0:T(8,128)S(1)} %is-finite_select_fusion), kind=kLoop, calls=%fused_computation.7 | loop fusion | flops 13947600 | bytes 18817440 | tf_op jit(solution)/shard_map/reduce_sum | solution.py:85
  169.8 10.0 %copy.73 = bf16[20,197,1,6,64]{1,4,3,0,2:T(8,128)(2,1)} copy(bf16[20,197,1,6,64]{4,3,2,1,0:T(8,128)(2,1)} %get-tuple-element.47) | data formatting | bytes 6051840
  179.8 15.8 %convert_bitcast_fusion = bf16[20,197,6,64]{1,3,2,0:T(8,128)(2,1)} fusion(bf16[20,197,1,6,64]{1,4,3,0,2:T(8,128)(2,1)} %copy.73, f32[20,6,197]{2,1,0:T(8,128)S(1)} %log_add_fusion, f32[20,6,197,197]{2,3,1,0:T(8,128)} %get-tuple-element.50), kind=kOutput, calls=%fused_computation.73 | convolution fusion | flops 611590464 | bytes 24774720 | tf_op jit(solution)/shard_map/bhst,bthe->bshe/dot_general | solution.py:87
  195.6 6.8 copy.57
  202.4 6.6 reshape.187
  209.1 6.0 all_gather.50
  215.1 5.4 fusion.68
  220.5 3.0 copy-done.2
  225.0 4.4 all-gather
  229.4 2.5 convert_element_type.129
  232.4 62.6 %fusion.4 = (bf16[3940,1536]{1,0:T(8,128)(2,1)}, f32[3940,1536]{1,0:T(8,128)}) fusion(f32[1536]{0:T(1024)S(1)} %reshape.219, bf16[384,1536]{1,0:T(8,128)(2,1)} %all-gather.4.cloned.1.call-done, f32[3940,384]{1,0:T(8,128)} %copy-done.2, f32[384]{0:T(512)S(1)} %convert_element_type.115, f32[384]{0:T(512)S(1)} %convert_element_type.114, ...), kind=kOutput, calls=%fused_computation.10 | convolution fusion | flops 5054799360 | bytes 43583264 | tf_op jit(solution)/shard_map/dot_general | solution.py:11
  295.1 20.8 %fusion.71 = (f32[1536]{0:T(1024)}, bf16[3940,1536]{1,0:T(8,128)(2,1)}) fusion(f32[3940,1536]{1,0:T(8,128)} %get-tuple-element.54, f32[1536]{0:T(1024)S(1)} %reshape.219, bf16[3940,384]{1,0:T(8,128)(2,1)S(1)} %copy-done.8, bf16[1536,384]{1,0:T(8,128)(2,1)} %all-gather.6.cloned.1.call-done), kind=kOutput, calls=%fused_computation.118 | convolution fusion | flops 4720433664 | bytes 40528896 | tf_op jit(solution)/shard_map/dot_general | solution.py:21
  315.8 11.3 %fusion.27 = f32[384,1536]{1,0:T(8,128)} fusion(bf16[3940,1536]{1,0:T(8,128)(2,1)} %get-tuple-element.62, f32[3940,384]{1,0:T(8,128)S(1)} %copy-done.3, f32[384]{0:T(512)S(1)} %convert_element_type.115, f32[384]{0:T(512)S(1)} %convert_element_type.114, f32[3940]{0:T(1024)S(1)} %add_rsqrt_fusion.1, f32[3940]{0:T(1024)S(1)} %broadcast_multiply_fusion.5), kind=kOutput, calls=%fused_computation.49 | convolution fusion | flops 4655377920 | bytes 20549408 | tf_op jit(solution)/shard_map/dot_general | solution.py:15
  327.2 10.6 %multiply_reduce_fusion.3 = (f32[384]{0:T(512)S(1)}, f32[3940]{0:T(1024)S(1)}, f32[3940]{0:T(1024)S(1)}, f32[384]{0:T(512)S(1)}, f32[3940,384]{1,0:T(8,128)S(1)}) fusion(f32[3940,384]{1,0:T(8,128)S(1)} %copy-done.3, f32[3940]{0:T(1024)S(1)} %add_rsqrt_fusion.1, f32[3940]{0:T(1024)S(1)} %broadcast_multiply_fusion.5, f32[384]{0:T(512)S(1)} %convert_element_type.114, ...), kind=kOutput, calls=%fused_computation.43 | convolution fusion | flops 4661420544 | bytes 25454656 | tf_op jit(solution)/shard_map/dot_general | solution.py:21
  337.8 3.6 fusion.66
  341.4 2.8 fusion.54
  346.6 7.4 %reshape.237 = bf16[20,197,6,64]{3,2,1,0:T(8,128)(2,1)} reshape(bf16[3940,384]{1,0:T(8,128)(2,1)S(1)} %convolution_convert_fusion) | data formatting | bytes 6051840 | tf_op jit(solution)/shard_map/reshape | solution.py:164
  354.0 9.9 %copy.59 = bf16[20,197,6,64]{1,3,2,0:T(8,128)(2,1)} copy(bf16[20,197,6,64]{3,2,1,0:T(8,128)(2,1)} %reshape.237) | data formatting | bytes 6051840 | tf_op jit(solution)/shard_map/reshape | solution.py:164
  363.9 14.9 %fusion.36 = f32[20,6,197,197]{2,3,1,0:T(8,128)} fusion(bf16[20,197,6,64]{1,3,2,0:T(8,128)(2,1)} %copy.59, bf16[20,197,1,6,64]{1,4,3,0,2:T(8,128)(2,1)} %copy.73), kind=kOutput, calls=%fused_computation.69 | convolution fusion | flops 596106240 | bytes 24680160 | tf_op jit(solution)/shard_map/bshe,bthe->bhst/dot_general | solution.py:170
  378.9 36.2 %bitcast_reduce_fusion.1 = (f32[6,64]{1,0:T(8,128)S(1)}, bf16[20,6,64,197]{3,2,1,0:T(8,128)(2,1)}) fusion(f32[20,6,197,197]{2,3,1,0:T(8,128)} %fusion.36, f32[20,6,197]{2,1,0:T(8,128)S(1)} %copy-done.15, f32[20,6,197,197]{2,3,1,0:T(8,128)} %get-tuple-element.50, bf16[20,197,1,6,64]{1,4,3,0,2:T(8,128)(2,1)} %copy.75), kind=kOutput, calls=%fused_computation.39 | convolution fusion | flops 641069312 | bytes 43404576 | tf_op jit(solution)/shard_map/bhst,bthe->bshe/dot_general | solution.py:175
  415.1 41.0 %fusion.40 = bf16[20,197,1,6,64]{1,4,3,0,2:T(8,128)(2,1)} fusion(f32[20,6,197,197]{2,3,1,0:T(8,128)} %fusion.36, f32[20,6,197]{2,1,0:T(8,128)S(1)} %copy-done.15, f32[20,6,197,197]{2,3,1,0:T(8,128)} %get-tuple-element.50, bf16[20,197,1,6,64]{1,4,3,0,2:T(8,128)(2,1)} %copy.74), kind=kOutput, calls=%fused_computation.74 | convolution fusion | flops 638043776 | bytes 43403040 | tf_op jit(solution)/shard_map/bhst,bshe->bthe/dot_general | solution.py:178
  456.1 13.8 %bitcast_reduce_fusion = (f32[6,64]{1,0:T(8,128)S(1)}, bf16[20,6,64,197]{3,2,1,0:T(8,128)(2,1)}) fusion(bf16[20,197,6,64]{1,3,2,0:T(8,128)(2,1)} %copy.59, f32[20,6,197]{2,1,0:T(8,128)S(1)} %copy-done.15, f32[20,6,197,197]{2,3,1,0:T(8,128)} %get-tuple-element.50), kind=kOutput, calls=%fused_computation.38 | convolution fusion | flops 613103040 | bytes 24776256 | tf_op jit(solution)/shard_map/bhst,bshe->bthe/dot_general | solution.py:167
  469.9 7.1 maximum_convert_fusion
  477.1 9.9 %copy.64 = bf16[20,197,3,6,64]{1,0,4,3,2:T(8,128)(2,1)} copy(bf16[20,197,3,6,64]{1,4,3,0,2:T(8,128)(2,1)S(1)} %maximum_convert_fusion) | data formatting | bytes 18155520 | tf_op jit(solution)/shard_map/convert_element_type | solution.py:186
  486.9 20.8 %convert_element_type.127 = bf16[3940,1152]{0,1:T(8,128)(2,1)} reshape(bf16[20,197,3,6,64]{1,0,4,3,2:T(8,128)(2,1)} %copy.64) | data formatting | bytes 18155520 | tf_op jit(solution)/shard_map/convert_element_type | solution.py:186
  507.8 13.7 %multiply_reduce_fusion.4 = (f32[384]{0:T(512)S(1)}, f32[3940]{0:T(1024)S(1)}, f32[3940]{0:T(1024)S(1)}, f32[384]{0:T(512)S(1)}, f32[3940,384]{1,0:T(8,128)}) fusion(f32[3940,384]{1,0:T(8,128)} %reshape.192, f32[3940]{0:T(1024)S(1)} %copy-done.24, f32[3940]{0:T(1024)S(1)} %copy-done.22, f32[384]{0:T(512)S(1)} %copy-done.26, ...), kind=kOutput, calls=%fused_computation.44 | convolution fusion | flops 3499467776 | bytes 22133824 | tf_op jit(solution)/shard_map/dot_general | solution.py:21
  521.5 5.6 fusion.72
  527.1 10.8 %fusion.73 = f32[1536,384]{1,0:T(8,128)} fusion(bf16[3940,1536]{1,0:T(8,128)(2,1)} %get-tuple-element.53, bf16[3940,384]{1,0:T(8,128)(2,1)S(1)} %copy-done.9), kind=kOutput, calls=%fused_computation.120 | convolution fusion | flops 4647813120 | bytes 17488896 | tf_op jit(solution)/shard_map/dot_general | solution.py:15
  537.9 11.0 %multiply_add_fusion = f32[3940,384]{1,0:T(8,128)} fusion(f32[3940,384]{1,0:T(8,128)} %copy-done, f32[3940,384]{1,0:T(8,128)} %get-tuple-element.56, f32[3940,384]{1,0:T(8,128)} %reshape.192, f32[3940]{0:T(1024)S(1)} %broadcast_multiply_fusion.1, f32[3940]{0:T(1024)S(1)} %broadcast_multiply_fusion.2, f32[384]{0:T(512)S(1)} %copy-done.26, ...), kind=kLoop, calls=%fused_computation.45 | loop fusion | flops 12103680 | bytes 24271936 | tf_op jit(solution)/shard_map/add | solution.py:193
  549.0 5.6 reshape.191
  554.6 10.8 %add_convert_fusion.1 = bf16[3940,384]{1,0:T(8,128)(2,1)S(1)} fusion(f32[3940,384]{1,0:T(8,128)} %copy-done.2, bf16[3940,1536]{1,0:T(8,128)(2,1)} %get-tuple-element.53, bf16[1536,384]{1,0:T(8,128)(2,1)} %all-gather.6.cloned.1.call-done, f32[384]{0:T(512)S(1)} %copy-done.30), kind=kOutput, calls=%fused_computation.53 | convolution fusion | flops 4652352000 | bytes 22362624 | tf_op jit(solution)/shard_map/dot_general | solution.py:11
  565.4 2.4 reshape.188
  567.9 39.7 %all-reduce.8 = (f32[384]{0:T(512)S(1)}, f32[384]{0:T(512)S(1)}, f32[384]{0:T(512)S(1)}, f32[384]{0:T(512)S(1)}, f32[384]{0:T(512)S(1)}, /*index=5*/f32[384]{0:T...) all-reduce(f32[384]{0:T(512)S(1)} %get-tuple-element.17, ...), channel_id=1, replica_groups=mesh['replica'=16,'group'=2] {'replica','group'}, use_global_device_ids=true, to_apply=%region_12.0 | all-reduce | flops 4608 | bytes 36864 | tf_op jit(solution)/shard_map/psum | solution.py:281
  613.3 89.2 %all-reduce.13.cloned.1.call-done = (f32[384,1152]{1,0:T(8,128)}, f32[384,384]{1,0:T(8,128)}, f32[384,1536]{1,0:T(8,128)}, f32[1536,384]{1,0:T(8,128)}) async-done(((f32[384,1152]{1,0:T(8,128)}, f32[384,384]{1,0:T(8,128)}, f32[384,1536]{1,0:T(8,128)}, f32[1536,384]{1,0:T(8,128)}), (f32[384,1152]{1,0:T(8,128)}, f32[384,384]{1,0:T(8,128)}, f32[384,1536]{1,0:T(8,128)}, ...) | async-done | bytes 7077904 | tf_op jit(solution)/shard_map/psum | solution.py:281
  702.5 2.4 dynamic-slice_multiply_fusion
  (141 shorter events, 41.4 us)
Async XLA Ops:
  7.2 4.2 copy-start.4
  7.2 225.3 %all-gather.4.cloned.1.call-start = ((), (), s32[]{:S(2)}) async-start(), calls=%async_computation | async-start | bytes 1769472 | tf_op jit(solution)/shard_map/all_gather | solution.py:244
  7.9 287.1 %all-gather.6.cloned.1.call-start = ((), (), s32[]{:S(2)}) async-start(), calls=%async_computation.1 | async-start | bytes 1769472 | tf_op jit(solution)/shard_map/all_gather | solution.py:246
  8.7 693.8 %all-reduce.13.cloned.1.call-start = ((), (), s32[]{:S(2)}) async-start(), calls=%async_computation.2 | async-start | bytes 14155776 | tf_op jit(solution)/shard_map/psum | solution.py:281
  13.7 58.4 %copy-start.21 = (f32[3940]{0:T(1024)}, f32[3940]{0:T(1024)S(1)}, u32[]{:S(2)}) copy-start(f32[3940]{0:T(1024)S(1)} %div.27) | copy-start | bytes 47284
  17.1 36.6 %copy-start.18 = (bf16[192,1152]{1,0:T(8,128)(2,1)S(1)}, bf16[192,1152]{1,0:T(8,128)(2,1)}, u32[]{:S(2)}) copy-start(bf16[192,1152]{1,0:T(8,128)(2,1)} %param.19) | copy-start | bytes 1327108
  53.7 18.4 %copy-start.36 = (bf16[384]{0:T(512)(128)(2,1)S(1)}, bf16[384]{0:T(512)(128)(2,1)}, u32[]{:S(2)}) copy-start(bf16[384]{0:T(512)(128)(2,1)} %get-tuple-element.36) | copy-start | bytes 2308
  53.7 18.4 %copy-start.37 = (bf16[384]{0:T(512)(128)(2,1)S(1)}, bf16[384]{0:T(512)(128)(2,1)}, u32[]{:S(2)}) copy-start(bf16[384]{0:T(512)(128)(2,1)} %get-tuple-element.37) | copy-start | bytes 2308
  53.7 18.5 %copy-start.1 = (f32[3940,384]{1,0:T(8,128)S(1)}, f32[3940,384]{1,0:T(8,128)}, u32[]{:S(2)}) copy-start(f32[3940,384]{1,0:T(8,128)} %reshape.192) | copy-start | bytes 18155524
  53.7 18.5 %copy-start.23 = (f32[3940]{0:T(1024)S(1)}, f32[3940]{0:T(1024)}, u32[]{:S(2)}) copy-start(f32[3940]{0:T(1024)} %rsqrt.21) | copy-start | bytes 47284
  53.7 18.5 %copy-start.25 = (f32[384]{0:T(512)S(1)}, f32[384]{0:T(512)}, u32[]{:S(2)}) copy-start(f32[384]{0:T(512)} %convert_element_type.105) | copy-start | bytes 4612
  53.7 18.5 %copy-start.27 = (f32[384]{0:T(512)S(1)}, f32[384]{0:T(512)}, u32[]{:S(2)}) copy-start(f32[384]{0:T(512)} %convert_element_type.106) | copy-start | bytes 4612
  68.8 3.4 copy-start.16
  169.8 25.8 %copy-start.14 = (f32[20,6,197]{2,1,0:T(8,128)}, f32[20,6,197]{2,1,0:T(8,128)S(1)}, u32[]{:S(2)}) copy-start(f32[20,6,197]{2,1,0:T(8,128)S(1)} %log_add_fusion) | copy-start | bytes 283684
  195.6 13.4 %copy-start.35 = (bf16[384]{0:T(512)(128)(2,1)S(1)}, bf16[384]{0:T(512)(128)(2,1)}, u32[]{:S(2)}) copy-start(bf16[384]{0:T(512)(128)(2,1)} %get-tuple-element.40) | copy-start | bytes 2308
  195.6 13.4 %copy-start.19 = (bf16[192,384]{1,0:T(8,128)(2,1)S(1)}, bf16[192,384]{1,0:T(8,128)(2,1)}, u32[]{:S(2)}) copy-start(bf16[192,384]{1,0:T(8,128)(2,1)} %param.22) | copy-start | bytes 442372
  209.0 11.4 %copy-start.5 = (bf16[3940,384]{0,1:T(8,128)(2,1)}, bf16[3940,384]{0,1:T(8,128)(2,1)S(1)}, u32[]{:S(2)}) copy-start(bf16[3940,384]{0,1:T(8,128)(2,1)S(1)} %reshape.187) | copy-start | bytes 9077764
  215.1 5.4 copy-start.12
  220.5 3.1 copy-start.2
  220.5 4.4 copy-start.34
  220.5 4.4 copy-start.33
  220.5 4.4 copy-start.31
  220.5 8.9 %copy-start.7 = (bf16[20,197,384]{2,1,0:T(8,128)(2,1)S(1)}, bf16[20,197,384]{2,1,0:T(8,128)(2,1)}, u32[]{:S(2)}) copy-start(bf16[20,197,384]{2,1,0:T(8,128)(2,1)} %add_convert_fusion) | copy-start | bytes 9077764
  223.5 8.3 %copy-start.32 = (bf16[384]{0:T(512)(128)(2,1)S(1)}, bf16[384]{0:T(512)(128)(2,1)}, u32[]{:S(2)}) copy-start(bf16[384]{0:T(512)(128)(2,1)} %get-tuple-element.43) | copy-start | bytes 2308
  232.4 62.6 %copy-start.8 = (bf16[3940,384]{1,0:T(8,128)(2,1)S(1)}, bf16[3940,384]{1,0:T(8,128)(2,1)}, u32[]{:S(2)}) copy-start(bf16[3940,384]{1,0:T(8,128)(2,1)} %reshape.189) | copy-start | bytes 9077764
  295.1 20.8 %copy-start.3 = (f32[3940,384]{1,0:T(8,128)S(1)}, f32[3940,384]{1,0:T(8,128)}, u32[]{:S(2)}) copy-start(f32[3940,384]{1,0:T(8,128)} %copy-done.2) | copy-start | bytes 18155524
  315.8 11.3 %copy-start.38 = (bf16[384,1536]{1,0:T(8,128)(2,1)S(1)}, bf16[384,1536]{1,0:T(8,128)(2,1)}, u32[]{:S(2)}) copy-start(bf16[384,1536]{1,0:T(8,128)(2,1)} %all-gather.4.cloned.1.call-done) | copy-start | bytes 3538948
  337.8 3.7 copy-start.6
  341.4 2.8 copy-start
  341.4 2.8 copy-start.13
  363.9 14.9 %copy-start.15 = (f32[20,6,197]{2,1,0:T(8,128)S(1)}, f32[20,6,197]{2,1,0:T(8,128)}, u32[]{:S(2)}) copy-start(f32[20,6,197]{2,1,0:T(8,128)} %copy-done.14) | copy-start | bytes 283684
  486.9 20.8 %copy-start.17 = (bf16[384,1152]{1,0:T(8,128)(2,1)S(1)}, bf16[384,1152]{1,0:T(8,128)(2,1)}, u32[]{:S(2)}) copy-start(bf16[384,1152]{1,0:T(8,128)(2,1)} %copy-done.16) | copy-start | bytes 2654212
  486.9 20.8 %copy-start.22 = (f32[3940]{0:T(1024)S(1)}, f32[3940]{0:T(1024)}, u32[]{:S(2)}) copy-start(f32[3940]{0:T(1024)} %copy-done.21) | copy-start | bytes 47284
  486.9 20.8 %copy-start.24 = (f32[3940]{0:T(1024)S(1)}, f32[3940]{0:T(1024)}, u32[]{:S(2)}) copy-start(f32[3940]{0:T(1024)} %rsqrt.21) | copy-start | bytes 47284
  486.9 20.8 %copy-start.26 = (f32[384]{0:T(512)S(1)}, f32[384]{0:T(512)}, u32[]{:S(2)}) copy-start(f32[384]{0:T(512)} %convert_element_type.105) | copy-start | bytes 4612
  507.8 13.7 %copy-start.10 = (bf16[3940,1152]{0,1:T(8,128)(2,1)S(1)}, bf16[3940,1152]{0,1:T(8,128)(2,1)}, u32[]{:S(2)}) copy-start(bf16[3940,1152]{0,1:T(8,128)(2,1)} %convert_element_type.127) | copy-start | bytes 27233284
  507.8 13.7 %copy-start.11 = (bf16[3940,384]{1,0:T(8,128)(2,1)S(1)}, bf16[3940,384]{1,0:T(8,128)(2,1)}, u32[]{:S(2)}) copy-start(bf16[3940,384]{1,0:T(8,128)(2,1)} %convert_element_type.129) | copy-start | bytes 9077764
  521.5 5.6 copy-start.9
  548.9 5.8 copy-start.30
  554.6 13.2 %copy-start.28 = (f32[1536]{0:T(1024)S(1)}, f32[1536]{0:T(1024)}, u32[]{:S(2)}) copy-start(f32[1536]{0:T(1024)} %get-tuple-element.61) | copy-start | bytes 18436
  554.6 13.2 %copy-start.29 = (f32[384]{0:T(512)S(1)}, f32[384]{0:T(512)}, u32[]{:S(2)}) copy-start(f32[384]{0:T(512)} %convert_reduce_fusion) | copy-start | bytes 4612
  702.5 7.0 copy-start.20
Sparse Core Ops, SparseCore 0:
  9.5 25.4 all-gather.3
  36.6 24.9 all-gather.5
  538.0 164.4 all-reduce.12
where the time goes:
time: 724 us; the launch traced here: 717 us
  matrix products  302 us (42%)
  local copies, waits for them, and re-layouts  174 us (24%)
  waiting for transfers between devices  90.6 us (13%)
  blocking collectives  71.9 us (10%)
  other arithmetic  62.9 us (9%)
  between operations  15.1 us (2%)
    psum x1, waiting for transfers between devices, local(): lax.psum((term_gain_one, term_shift_one, term_w_qkv, term_b_query, term_b...  89.2 us
    dot_general x4, matrix products, product(): return jnp.dot(left, right, preferred_element_type=jnp.float32)  87.4 us
    unnamed x100, local copies, waits for them, and re-layouts  49 us
    dot_general x4, matrix products, product_right_t(): lax.dot_general(left, right, (((1,), (1,)), ((), ())), preferred_element_...  47.4 us
    dot_general x1, matrix products, backward_pass(): jnp.einsum('bhst,bshe->bthe', grad_scores, query, preferred_element_type=...  41 us
    psum x1, blocking collectives, local(): lax.psum((term_gain_one, term_shift_one, term_w_qkv, term_b_query, term_b...  39.7 us
    dot_general x1, matrix products, backward_pass(): jnp.einsum('bhst,bthe->bshe', grad_scores, keys, preferred_element_type=j...  36.2 us
    convert_element_type x2, local copies, waits for them, and re-layouts, backward_pass(): grad_packed_b = jnp.stack([grad_query, grad_keys, grad_values], axis=2).r...  30.7 us
  transfers between devices with their start and end apart: 3, of which 1 were waited for; matrix products, arithmetic and copies ran while one was open for 40% of the time, Pallas kernels for 0%

commit v1 on v0

--- a/solution.py
+++ b/solution.py
@@ -279,22 +279,25 @@
         term_b_fc2,
     ) = grads
     wholes = lax.psum(
-        (
-            term_gain_one,
-            term_shift_one,
-            term_w_qkv,
-            term_b_query,
-            term_b_value,
-            term_w_proj,
-            term_b_proj,
-            term_gain_two,
-            term_shift_two,
-            term_w_fc1,
-            term_b_fc1,
-            term_w_fc2,
-            term_b_fc2,
+        lax.psum(
+            (
+                term_gain_one,
+                term_shift_one,
+                term_w_qkv,
+                term_b_query,
+                term_b_value,
+                term_w_proj,
+                term_b_proj,
+                term_gain_two,
+                term_shift_two,
+                term_w_fc1,
+                term_b_fc1,
+                term_w_fc2,
+                term_b_fc2,
+            ),
+            "group",
         ),
-        ("replica", "group"),
+        "replica",
     )
     position = lax.axis_index("group")
     members = lax.axis_size("group")

time: 724 us -> 873 us (1.21)
  waiting for transfers between devices: 90.6 us -> 205 us
  blocking collectives: 71.9 us -> 109 us
    psum x1, waiting for transfers between devices: 89.2 us -> 153 us  [local(): lax.psum((term_gain_one, term_shift_one, term_w_qkv, term_b_query, term_b...]
    psum x0 -> x1, blocking collectives: none -> 61.7 us  [local(): lax.psum(lax.psum((term_gain_one, term_shift_one, term_w_qkv, term_b_quer...]
    psum x0 -> x1, waiting for transfers between devices: none -> 50.8 us  [local(): lax.psum(lax.psum((term_gain_one, term_shift_one, term_w_qkv, term_b_quer...]
    psum x1, blocking collectives: 39.7 us -> 7.41 us  [local(): lax.psum((term_gain_one, term_shift_one, term_w_qkv, term_b_query, term_b...]
    unnamed x100 -> x96, local copies, waits for them, and re-layouts: 49 us -> 50.7 us
  transfers between devices with their start and end apart: 3 -> 4, of which waited for: 1 -> 2; matrix products, arithmetic and copies ran while one was open for 40% -> 34% of each run, Pallas kernels for 0% -> 0%
where the time goes in v1:
time: 873 us; the launch traced here: 867 us
  matrix products  303 us (35%)
  waiting for transfers between devices  205 us (23%)
  local copies, waits for them, and re-layouts  176 us (20%)
  blocking collectives  109 us (12%)
  other arithmetic  59 us (7%)
  between operations  15.4 us (2%)
    psum x1, waiting for transfers between devices, local(): lax.psum((term_gain_one, term_shift_one, term_w_qkv, term_b_query, term_b...  153 us
    dot_general x4, matrix products, product(): return jnp.dot(left, right, preferred_element_type=jnp.float32)  86.9 us
    psum x1, blocking collectives, local(): lax.psum(lax.psum((term_gain_one, term_shift_one, term_w_qkv, term_b_quer...  61.7 us
    psum x1, waiting for transfers between devices, local(): lax.psum(lax.psum((term_gain_one, term_shift_one, term_w_qkv, term_b_quer...  50.8 us
    unnamed x96, local copies, waits for them, and re-layouts  50.7 us
    dot_general x4, matrix products, product_right_t(): lax.dot_general(left, right, (((1,), (1,)), ((), ())), preferred_element_...  48.8 us
    dot_general x1, matrix products, backward_pass(): jnp.einsum('bhst,bshe->bthe', grad_scores, query, preferred_element_type=...  41 us
    dot_general x1, matrix products, backward_pass(): jnp.einsum('bhst,bthe->bshe', grad_scores, keys, preferred_element_type=j...  36.2 us
  transfers between devices with their start and end apart: 4, of which 2 were waited for; matrix products, arithmetic and copies ran while one was open for 34% of the time, Pallas kernels for 0%

profile of v1, /device:TPU:0, one launch (start us, length us, event | category | flops | bytes accessed | tf_op | source)
XLA Modules:
  0.0 867.2 jit_solution(2639844314006322271)
XLA Ops:
  8.7 2.6 convert_reduce_fusion.1
  13.7 3.3 reshape.192
  34.2 6.7 all-reduce.12
  46.2 22.4 %all_gather.47 = bf16[384,1152]{1,0:T(8,128)(2,1)S(1)} all-gather(bf16[192,1152]{1,0:T(8,128)(2,1)S(1)} %copy-done.18), channel_id=1, replica_groups=mesh['replica'=16,'group'=2] {'group'}, dimensions={0}, use_global_device_ids=true | all-gather | bytes 1327104 | tf_op jit(solution)/shard_map/all_gather | solution.py:237
  68.6 3.3 add_convert_fusion
  72.1 8.7 %fusion.17 = bf16[3940,1152]{1,0:T(8,128)(2,1)} fusion(bf16[384,1152]{1,0:T(8,128)(2,1)S(1)} %all_gather.47, f32[1152]{0:T(1024)S(1)} %maximum_convert_fusion.1, f32[3940,384]{1,0:T(8,128)S(1)} %copy-done.1, f32[384]{0:T(512)S(1)} %copy-done.27, f32[384]{0:T(512)S(1)} %copy-done.25, f32[3940]{0:T(1024)S(1)} %copy-done.23, f32[3940]{0:T(1024)S(1)} %div.27), kind=kOutput, calls=%fused_computation.34 | convolution fusion | flops 3502502400 | bytes 16053536 | tf_op jit(solution)/shard_map/dot_general | solution.py:11
  80.7 27.6 %reshape.236 = bf16[20,197,3,6,64]{4,3,2,1,0:T(8,128)(2,1)} reshape(bf16[3940,1152]{1,0:T(8,128)(2,1)} %fusion.17) | data formatting | bytes 18155520 | tf_op jit(solution)/shard_map/reshape | solution.py:80
  108.4 16.3 %fusion.67 = (bf16[20,197,1,6,64]{4,3,2,1,0:T(8,128)(2,1)}, bf16[20,197,1,6,64]{4,3,2,1,0:T(8,128)(2,1)}, bf16[20,197,1,6,64]{4,3,2,1,0:T(8,128)(2,1)}) fusion(bf16[20,197,3,6,64]{4,3,2,1,0:T(8,128)(2,1)} %reshape.236), kind=kLoop, calls=%fused_computation.116 | loop fusion | bytes 18155520 | tf_op jit(solution)/shard_map/slice | solution.py:81
  124.7 9.7 %copy.74 = bf16[20,197,1,6,64]{1,4,3,0,2:T(8,128)(2,1)} copy(bf16[20,197,1,6,64]{4,3,2,1,0:T(8,128)(2,1)} %get-tuple-element.59) | data formatting | bytes 6051840
  134.4 9.7 %copy.75 = bf16[20,197,1,6,64]{1,4,3,0,2:T(8,128)(2,1)} copy(bf16[20,197,1,6,64]{4,3,2,1,0:T(8,128)(2,1)} %get-tuple-element.61) | data formatting | bytes 6051840
  144.1 14.9 %multiply_reduce_fusion.1 = (f32[20,6,197]{2,1,0:T(8,128)S(1)}, f32[20,6,197,197]{2,3,1,0:T(8,128)}) fusion(bf16[20,197,1,6,64]{1,4,3,0,2:T(8,128)(2,1)} %copy.75, bf16[20,197,1,6,64]{1,4,3,0,2:T(8,128)(2,1)} %copy.74), kind=kOutput, calls=%fused_computation.32 | convolution fusion | flops 605396736 | bytes 24774720 | tf_op jit(solution)/shard_map/bshe,bthe->bhst/dot_general | solution.py:53
  159.0 10.6 %exponential_reduce_fusion = f32[20,6,197]{2,1,0:T(8,128)S(1)} fusion(f32[20,6,197,197]{2,3,1,0:T(8,128)} %get-tuple-element.63, f32[20,6,197]{2,1,0:T(8,128)S(1)} %is-finite_select_fusion), kind=kLoop, calls=%fused_computation.7 | loop fusion | flops 13947600 | bytes 18817440 | tf_op jit(solution)/shard_map/reduce_sum | solution.py:85
  169.7 9.9 %copy.73 = bf16[20,197,1,6,64]{1,4,3,0,2:T(8,128)(2,1)} copy(bf16[20,197,1,6,64]{4,3,2,1,0:T(8,128)(2,1)} %get-tuple-element.60) | data formatting | bytes 6051840
  179.6 15.8 %convert_bitcast_fusion = bf16[20,197,6,64]{1,3,2,0:T(8,128)(2,1)} fusion(bf16[20,197,1,6,64]{1,4,3,0,2:T(8,128)(2,1)} %copy.73, f32[20,6,197]{2,1,0:T(8,128)S(1)} %log_add_fusion, f32[20,6,197,197]{2,3,1,0:T(8,128)} %get-tuple-element.63), kind=kOutput, calls=%fused_computation.73 | convolution fusion | flops 611590464 | bytes 24774720 | tf_op jit(solution)/shard_map/bhst,bthe->bshe/dot_general | solution.py:87
  195.4 6.8 copy.57
  202.2 6.6 reshape.187
  208.9 5.8 all_gather.50
  214.7 5.4 fusion.68
  220.1 3.0 copy-done.2
  224.5 4.6 all-gather
  229.2 2.4 reshape.189
  231.6 4.2 convert_element_type.129
  235.9 62.0 %fusion.4 = (bf16[3940,1536]{1,0:T(8,128)(2,1)}, f32[3940,1536]{1,0:T(8,128)}) fusion(f32[1536]{0:T(1024)S(1)} %reshape.219, bf16[384,1536]{1,0:T(8,128)(2,1)} %all-gather.4.cloned.1.call-done, f32[3940,384]{1,0:T(8,128)} %copy-done.2, f32[384]{0:T(512)S(1)} %convert_element_type.115, f32[384]{0:T(512)S(1)} %convert_element_type.114, ...), kind=kOutput, calls=%fused_computation.10 | convolution fusion | flops 5054799360 | bytes 43583264 | tf_op jit(solution)/shard_map/dot_general | solution.py:11
  297.9 20.8 %fusion.71 = (f32[1536]{0:T(1024)}, bf16[3940,1536]{1,0:T(8,128)(2,1)}) fusion(f32[3940,1536]{1,0:T(8,128)} %get-tuple-element.67, f32[1536]{0:T(1024)S(1)} %reshape.219, bf16[3940,384]{1,0:T(8,128)(2,1)S(1)} %copy-done.9, bf16[1536,384]{1,0:T(8,128)(2,1)} %all-gather.6.cloned.1.call-done), kind=kOutput, calls=%fused_computation.118 | convolution fusion | flops 4720433664 | bytes 40528896 | tf_op jit(solution)/shard_map/dot_general | solution.py:21
  318.7 11.3 %fusion.27 = f32[384,1536]{1,0:T(8,128)} fusion(bf16[3940,1536]{1,0:T(8,128)(2,1)} %get-tuple-element.75, f32[3940,384]{1,0:T(8,128)S(1)} %copy-done.3, f32[384]{0:T(512)S(1)} %convert_element_type.115, f32[384]{0:T(512)S(1)} %convert_element_type.114, f32[3940]{0:T(1024)S(1)} %add_rsqrt_fusion.1, f32[3940]{0:T(1024)S(1)} %broadcast_multiply_fusion.5), kind=kOutput, calls=%fused_computation.49 | convolution fusion | flops 4655377920 | bytes 20549408 | tf_op jit(solution)/shard_map/dot_general | solution.py:15
  330.0 11.0 %multiply_reduce_fusion.3 = (f32[384]{0:T(512)S(1)}, f32[3940]{0:T(1024)S(1)}, f32[3940]{0:T(1024)S(1)}, f32[384]{0:T(512)S(1)}, f32[3940,384]{1,0:T(8,128)S(1)}) fusion(f32[3940,384]{1,0:T(8,128)S(1)} %copy-done.3, f32[3940]{0:T(1024)S(1)} %add_rsqrt_fusion.1, f32[3940]{0:T(1024)S(1)} %broadcast_multiply_fusion.5, f32[384]{0:T(512)S(1)} %convert_element_type.114, ...), kind=kOutput, calls=%fused_computation.43 | convolution fusion | flops 4661420544 | bytes 25454656 | tf_op jit(solution)/shard_map/dot_general | solution.py:21
  341.0 3.4 fusion.66
  344.5 2.8 fusion.54
  349.7 7.4 reshape.237
  357.0 9.9 %copy.59 = bf16[20,197,6,64]{1,3,2,0:T(8,128)(2,1)} copy(bf16[20,197,6,64]{3,2,1,0:T(8,128)(2,1)} %reshape.237) | data formatting | bytes 6051840 | tf_op jit(solution)/shard_map/reshape | solution.py:164
  367.0 14.9 %fusion.36 = f32[20,6,197,197]{2,3,1,0:T(8,128)} fusion(bf16[20,197,6,64]{1,3,2,0:T(8,128)(2,1)} %copy.59, bf16[20,197,1,6,64]{1,4,3,0,2:T(8,128)(2,1)} %copy.73), kind=kOutput, calls=%fused_computation.69 | convolution fusion | flops 596106240 | bytes 24680160 | tf_op jit(solution)/shard_map/bshe,bthe->bhst/dot_general | solution.py:170
  381.9 36.2 %bitcast_reduce_fusion.1 = (f32[6,64]{1,0:T(8,128)S(1)}, bf16[20,6,64,197]{3,2,1,0:T(8,128)(2,1)}) fusion(f32[20,6,197,197]{2,3,1,0:T(8,128)} %fusion.36, f32[20,6,197]{2,1,0:T(8,128)S(1)} %copy-done.16, f32[20,6,197,197]{2,3,1,0:T(8,128)} %get-tuple-element.63, bf16[20,197,1,6,64]{1,4,3,0,2:T(8,128)(2,1)} %copy.75), kind=kOutput, calls=%fused_computation.39 | convolution fusion | flops 641069312 | bytes 43404576 | tf_op jit(solution)/shard_map/bhst,bthe->bshe/dot_general | solution.py:175
  418.1 41.0 %fusion.40 = bf16[20,197,1,6,64]{1,4,3,0,2:T(8,128)(2,1)} fusion(f32[20,6,197,197]{2,3,1,0:T(8,128)} %fusion.36, f32[20,6,197]{2,1,0:T(8,128)S(1)} %copy-done.16, f32[20,6,197,197]{2,3,1,0:T(8,128)} %get-tuple-element.63, bf16[20,197,1,6,64]{1,4,3,0,2:T(8,128)(2,1)} %copy.74), kind=kOutput, calls=%fused_computation.74 | convolution fusion | flops 638043776 | bytes 43403040 | tf_op jit(solution)/shard_map/bhst,bshe->bthe/dot_general | solution.py:178
  459.2 13.8 %bitcast_reduce_fusion = (f32[6,64]{1,0:T(8,128)S(1)}, bf16[20,6,64,197]{3,2,1,0:T(8,128)(2,1)}) fusion(bf16[20,197,6,64]{1,3,2,0:T(8,128)(2,1)} %copy.59, f32[20,6,197]{2,1,0:T(8,128)S(1)} %copy-done.16, f32[20,6,197,197]{2,3,1,0:T(8,128)} %get-tuple-element.63), kind=kOutput, calls=%fused_computation.38 | convolution fusion | flops 613103040 | bytes 24776256 | tf_op jit(solution)/shard_map/bhst,bshe->bthe/dot_general | solution.py:167
  473.0 6.9 maximum_convert_fusion
  479.9 9.9 %copy.64 = bf16[20,197,3,6,64]{1,0,4,3,2:T(8,128)(2,1)} copy(bf16[20,197,3,6,64]{1,4,3,0,2:T(8,128)(2,1)S(1)} %maximum_convert_fusion) | data formatting | bytes 18155520 | tf_op jit(solution)/shard_map/convert_element_type | solution.py:186
  489.8 20.9 %convert_element_type.127 = bf16[3940,1152]{0,1:T(8,128)(2,1)} reshape(bf16[20,197,3,6,64]{1,0,4,3,2:T(8,128)(2,1)} %copy.64) | data formatting | bytes 18155520 | tf_op jit(solution)/shard_map/convert_element_type | solution.py:186
  510.6 10.8 %fusion.73 = f32[1536,384]{1,0:T(8,128)} fusion(bf16[3940,1536]{1,0:T(8,128)(2,1)} %get-tuple-element.66, bf16[3940,384]{1,0:T(8,128)(2,1)S(1)} %copy-done.10), kind=kOutput, calls=%fused_computation.120 | convolution fusion | flops 4647813120 | bytes 17488896 | tf_op jit(solution)/shard_map/dot_general | solution.py:15
  521.4 5.6 fusion.72
  529.5 14.7 %multiply_reduce_fusion.4 = (f32[384]{0:T(512)S(1)}, f32[3940]{0:T(1024)S(1)}, f32[3940]{0:T(1024)S(1)}, f32[384]{0:T(512)S(1)}, f32[3940,384]{1,0:T(8,128)}) fusion(f32[3940,384]{1,0:T(8,128)} %reshape.192, f32[3940]{0:T(1024)S(1)} %copy-done.24, f32[3940]{0:T(1024)S(1)} %copy-done.22, f32[384]{0:T(512)S(1)} %copy-done.26, ...), kind=kOutput, calls=%fused_computation.44 | convolution fusion | flops 3499467776 | bytes 22133824 | tf_op jit(solution)/shard_map/dot_general | solution.py:21
  544.2 153.3 %all-reduce.18.cloned.1.call-done = (f32[384,1152]{1,0:T(8,128)}, f32[384,384]{1,0:T(8,128)}, f32[384,1536]{1,0:T(8,128)}, f32[1536,384]{1,0:T(8,128)}) async-done(((f32[384,1152]{1,0:T(8,128)}, f32[384,384]{1,0:T(8,128)}, f32[384,1536]{1,0:T(8,128)}, f32[1536,384]{1,0:T(8,128)}), (f32[384,1152]{1,0:T(8,128)}, f32[384,384]{1,0:T(8,128)}, f32[384,1536]{1,0:T(8,128)}, ...) | async-done | bytes 7077904 | tf_op jit(solution)/shard_map/psum | solution.py:282
  697.5 10.4 %multiply_add_fusion = f32[3940,384]{1,0:T(8,128)} fusion(f32[3940,384]{1,0:T(8,128)} %copy-done, f32[3940,384]{1,0:T(8,128)} %get-tuple-element.69, f32[3940,384]{1,0:T(8,128)} %reshape.192, f32[3940]{0:T(1024)S(1)} %broadcast_multiply_fusion.1, f32[3940]{0:T(1024)S(1)} %broadcast_multiply_fusion.2, f32[384]{0:T(512)S(1)} %copy-done.26, ...), kind=kLoop, calls=%fused_computation.45 | loop fusion | flops 12103680 | bytes 24271936 | tf_op jit(solution)/shard_map/add | solution.py:193
  708.1 5.5 reshape.191
  713.5 10.8 %add_convert_fusion.1 = bf16[3940,384]{1,0:T(8,128)(2,1)S(1)} fusion(f32[3940,384]{1,0:T(8,128)} %copy-done.2, bf16[3940,1536]{1,0:T(8,128)(2,1)} %get-tuple-element.66, bf16[1536,384]{1,0:T(8,128)(2,1)} %all-gather.6.cloned.1.call-done, f32[384]{0:T(512)S(1)} %convert_element_type.119), kind=kOutput, calls=%fused_computation.53 | convolution fusion | flops 4652352000 | bytes 22362624 | tf_op jit(solution)/shard_map/dot_general | solution.py:11
  726.8 7.4 all-reduce.10
  734.2 61.7 %all-reduce.8 = (f32[384]{0:T(512)S(1)}, f32[384]{0:T(512)S(1)}, f32[384]{0:T(512)S(1)}, f32[384]{0:T(512)S(1)}, f32[384]{0:T(512)S(1)}, /*index=5*/f32[384]{0:T...) all-reduce(f32[384]{0:T(512)S(1)} %get-tuple-element.36, ...), channel_id=1, replica_groups=mesh['replica'=16,'group'=2] {'replica'}, use_global_device_ids=true, to_apply=%region_13.0 | all-reduce | flops 4608 | bytes 36864 | tf_op jit(solution)/shard_map/psum | solution.py:281
  801.7 50.8 %all-reduce.16.cloned.1.call-done = (f32[384,1152]{1,0:T(8,128)}, f32[384,384]{1,0:T(8,128)}, f32[384,1536]{1,0:T(8,128)}, f32[1536,384]{1,0:T(8,128)}) async-done(((f32[384,1152]{1,0:T(8,128)}, f32[384,384]{1,0:T(8,128)}, f32[384,1536]{1,0:T(8,128)}, f32[1536,384]{1,0:T(8,128)}), (f32[384,1152]{1,0:T(8,128)}, f32[384,384]{1,0:T(8,128)}, f32[384,1536]{1,0:T(8,128)}, ...) | async-done | bytes 7077904 | tf_op jit(solution)/shard_map/psum | solution.py:281
  852.5 2.4 dynamic-slice_multiply_fusion
  (141 shorter events, 45.6 us)
Async XLA Ops:
  7.2 4.2 copy-start.4
  7.2 228.7 %all-gather.4.cloned.1.call-start = ((), (), s32[]{:S(2)}) async-start(), calls=%async_computation | async-start | bytes 1769472 | tf_op jit(solution)/shard_map/all_gather | solution.py:244
  7.9 290.0 %all-gather.6.cloned.1.call-start = ((), (), s32[]{:S(2)}) async-start(), calls=%async_computation.1 | async-start | bytes 1769472 | tf_op jit(solution)/shard_map/all_gather | solution.py:246
  8.7 688.8 %all-reduce.18.cloned.1.call-start = ((), (), s32[]{:S(2)}) async-start(), calls=%async_computation.3 | async-start | bytes 14155776 | tf_op jit(solution)/shard_map/psum | solution.py:282
  11.4 34.8 %copy-start.18 = (bf16[192,1152]{1,0:T(8,128)(2,1)S(1)}, bf16[192,1152]{1,0:T(8,128)(2,1)}, u32[]{:S(2)}) copy-start(bf16[192,1152]{1,0:T(8,128)(2,1)} %param.19) | copy-start | bytes 1327108
  13.7 58.3 %copy-start.21 = (f32[3940]{0:T(1024)}, f32[3940]{0:T(1024)S(1)}, u32[]{:S(2)}) copy-start(f32[3940]{0:T(1024)S(1)} %div.27) | copy-start | bytes 47284
  46.2 25.8 %copy-start.34 = (bf16[384]{0:T(512)(128)(2,1)S(1)}, bf16[384]{0:T(512)(128)(2,1)}, u32[]{:S(2)}) copy-start(bf16[384]{0:T(512)(128)(2,1)} %get-tuple-element.49) | copy-start | bytes 2308
  46.2 25.8 %copy-start.35 = (bf16[384]{0:T(512)(128)(2,1)S(1)}, bf16[384]{0:T(512)(128)(2,1)}, u32[]{:S(2)}) copy-start(bf16[384]{0:T(512)(128)(2,1)} %get-tuple-element.50) | copy-start | bytes 2308
  46.2 25.8 %copy-start.1 = (f32[3940,384]{1,0:T(8,128)S(1)}, f32[3940,384]{1,0:T(8,128)}, u32[]{:S(2)}) copy-start(f32[3940,384]{1,0:T(8,128)} %reshape.192) | copy-start | bytes 18155524
  46.2 25.8 %copy-start.23 = (f32[3940]{0:T(1024)S(1)}, f32[3940]{0:T(1024)}, u32[]{:S(2)}) copy-start(f32[3940]{0:T(1024)} %rsqrt.21) | copy-start | bytes 47284
  46.2 25.8 %copy-start.25 = (f32[384]{0:T(512)S(1)}, f32[384]{0:T(512)}, u32[]{:S(2)}) copy-start(f32[384]{0:T(512)} %convert_element_type.105) | copy-start | bytes 4612
  46.2 25.8 %copy-start.27 = (f32[384]{0:T(512)S(1)}, f32[384]{0:T(512)}, u32[]{:S(2)}) copy-start(f32[384]{0:T(512)} %convert_element_type.106) | copy-start | bytes 4612
  68.6 3.4 copy-start.17
  169.6 25.8 %copy-start.15 = (f32[20,6,197]{2,1,0:T(8,128)}, f32[20,6,197]{2,1,0:T(8,128)S(1)}, u32[]{:S(2)}) copy-start(f32[20,6,197]{2,1,0:T(8,128)S(1)} %log_add_fusion) | copy-start | bytes 283684
  195.4 13.4 %copy-start.33 = (bf16[384]{0:T(512)(128)(2,1)S(1)}, bf16[384]{0:T(512)(128)(2,1)}, u32[]{:S(2)}) copy-start(bf16[384]{0:T(512)(128)(2,1)} %get-tuple-element.53) | copy-start | bytes 2308
  195.4 13.4 %copy-start.19 = (bf16[192,384]{1,0:T(8,128)(2,1)S(1)}, bf16[192,384]{1,0:T(8,128)(2,1)}, u32[]{:S(2)}) copy-start(bf16[192,384]{1,0:T(8,128)(2,1)} %param.22) | copy-start | bytes 442372
  208.8 11.2 %copy-start.5 = (bf16[3940,384]{0,1:T(8,128)(2,1)}, bf16[3940,384]{0,1:T(8,128)(2,1)S(1)}, u32[]{:S(2)}) copy-start(bf16[3940,384]{0,1:T(8,128)(2,1)S(1)} %reshape.187) | copy-start | bytes 9077764
  214.7 5.4 copy-start.13
  220.0 3.1 copy-start.2
  220.1 4.4 copy-start.32
  220.1 4.4 copy-start.31
  220.1 4.4 copy-start.29
  220.1 9.1 %copy-start.7 = (bf16[20,197,384]{2,1,0:T(8,128)(2,1)S(1)}, bf16[20,197,384]{2,1,0:T(8,128)(2,1)}, u32[]{:S(2)}) copy-start(bf16[20,197,384]{2,1,0:T(8,128)(2,1)} %param.16) | copy-start | bytes 9077764
  235.9 62.1 %copy-start.9 = (bf16[3940,384]{1,0:T(8,128)(2,1)S(1)}, bf16[3940,384]{1,0:T(8,128)(2,1)}, u32[]{:S(2)}) copy-start(bf16[3940,384]{1,0:T(8,128)(2,1)} %reshape.189) | copy-start | bytes 9077764
  297.9 20.8 %copy-start.3 = (f32[3940,384]{1,0:T(8,128)S(1)}, f32[3940,384]{1,0:T(8,128)}, u32[]{:S(2)}) copy-start(f32[3940,384]{1,0:T(8,128)} %copy-done.2) | copy-start | bytes 18155524
  318.7 11.3 %copy-start.36 = (bf16[384,1536]{1,0:T(8,128)(2,1)S(1)}, bf16[384,1536]{1,0:T(8,128)(2,1)}, u32[]{:S(2)}) copy-start(bf16[384,1536]{1,0:T(8,128)(2,1)} %all-gather.4.cloned.1.call-done) | copy-start | bytes 3538948
  341.0 3.5 copy-start.6
  344.5 2.8 copy-start
  344.5 2.8 copy-start.14
  367.0 14.9 %copy-start.16 = (f32[20,6,197]{2,1,0:T(8,128)S(1)}, f32[20,6,197]{2,1,0:T(8,128)}, u32[]{:S(2)}) copy-start(f32[20,6,197]{2,1,0:T(8,128)} %copy-done.15) | copy-start | bytes 283684
  489.8 20.9 %copy-start.10 = (bf16[3940,384]{1,0:T(8,128)(2,1)S(1)}, bf16[3940,384]{1,0:T(8,128)(2,1)}, u32[]{:S(2)}) copy-start(bf16[3940,384]{1,0:T(8,128)(2,1)} %reshape.189) | copy-start | bytes 9077764
  510.6 10.8 %copy-start.11 = (bf16[3940,1152]{0,1:T(8,128)(2,1)S(1)}, bf16[3940,1152]{0,1:T(8,128)(2,1)}, u32[]{:S(2)}) copy-start(bf16[3940,1152]{0,1:T(8,128)(2,1)} %convert_element_type.127) | copy-start | bytes 27233284
  510.6 10.8 %copy-start.12 = (bf16[3940,384]{1,0:T(8,128)(2,1)S(1)}, bf16[3940,384]{1,0:T(8,128)(2,1)}, u32[]{:S(2)}) copy-start(bf16[3940,384]{1,0:T(8,128)(2,1)} %convert_element_type.129) | copy-start | bytes 9077764
  527.0 0.7 copy-start.30
  527.0 1.9 copy-start.8
  527.0 2.4 copy-start.22
  527.0 2.4 copy-start.24
  527.0 2.5 copy-start.26
  527.1 325.4 %all-reduce.16.cloned.1.call-start = ((), (), s32[]{:S(2)}) async-start(), calls=%async_computation.2 | async-start | bytes 14155776 | tf_op jit(solution)/shard_map/psum | solution.py:281
  713.5 13.3 %copy-start.28 = (f32[1536]{0:T(1024)S(1)}, f32[1536]{0:T(1024)}, u32[]{:S(2)}) copy-start(f32[1536]{0:T(1024)} %get-tuple-element.74) | copy-start | bytes 18436
  852.5 7.0 copy-start.20
Sparse Core Ops, SparseCore 0:
  9.5 25.4 all-gather.3
  36.6 31.9 all-gather.5
  527.2 170.2 all-reduce.17
  701.4 151.0 all-reduce.15
